TPU v7x, 256 devices: a whole 4x4x8 slice. The times are simulated.
256 devices in a mesh: row: 4 (over x), col: 8 (over z), depth: 8 (over y, core).
Axes of the slice: x: 4, y: 4, z: 8, core: 2. Of those that a mesh axis runs over, the one named last changes fastest.
Arguments:
- trailing: float32 [1504, 48128], P('depth', ('row', 'col')), may hold values from -6 to 6
- panel_block: float32 [48128, 1024], P(('row', 'col', 'depth')), may hold values from -6 to 6
- factor_panel: float32 [48128, 1024], P(('row', 'col', 'depth')), may hold values from -0.1875 to 0.1875
- corner_block: float32 [1024, 1024], P(('row', 'col', 'depth')), may hold values from -6 to 6, as said below
- corner_inverse: float32 [1024, 1024], P(('row', 'col', 'depth')), may hold values from -1 to 2, as said below
Outputs:
- trailing_out: float32 [1504, 48128], P('depth', ('row', 'col'))
- panel_out: float32 [48128, 1024], P(('row', 'col', 'depth'))
- corner_out: float32 [1024, 1024], P(('row', 'col', 'depth'))
Inputs may be any that keep to these rules, and one draw needn't show every extreme that they name: `corner_block`: symmetric. `corner_inverse`: lower triangular, diagonal between 1 and 2.
All inputs are finite; a program needn't handle non-finite values.
Results may differ from a plain program's by a relative error of at most 0.00012.
Values sent between devices are 32-bit elements; how exact they have to be, the bound alone decides.
A program may use at most 128 MiB of HBM per device.

v0:
```python
import jax
import jax.numpy as jnp
from jax import lax
from jax.sharding import PartitionSpec as P


def sent_together(arrays, axis, dim, along):
    ends, at = ([], 0)
    for a in arrays[:-1]:
        at += a.shape[along]
        ends.append(at)
    both = jnp.concatenate(arrays, axis=along)
    return tuple(jnp.split(lax.all_gather(both, axis, axis=dim, tiled=True), ends, axis=along))


def spread(array, axes, root):
    array = jnp.where(lax.axis_index(axes) == root, array, jnp.zeros_like(array))
    for axis in axes:
        array = lax.psum(array, axis)
    return array


def matmul(left, right):
    return jnp.dot(left, right, precision=lax.Precision.HIGHEST, preferred_element_type=jnp.float32)


def contract(left, right):
    return lax.dot_general(
        left,
        right,
        (((1,), (1,)), ((), ())),
        precision=lax.Precision.HIGHEST,
        preferred_element_type=jnp.float32,
    )


def body(trailing, panel_block, factor_panel, corner_block, corner_inverse):
    corner_rows = corner_block.shape[0]
    whole_inverse, whole_corner = sent_together(
        (corner_inverse, corner_block), ("row", "col", "depth"), 0, 1
    )
    corner_full = matmul(whole_inverse, contract(whole_corner, whole_inverse))
    scaled = contract(panel_block, whole_inverse)
    coupling = matmul(factor_panel, corner_full)
    corner_out = lax.dynamic_slice_in_dim(
        corner_full, lax.axis_index(("row", "col", "depth")) * corner_rows, corner_rows, 0
    )
    half_panel = scaled - 0.5 * coupling
    panel_out = half_panel - 0.5 * coupling
    half_cols, lower_cols = (
        lax.all_gather(half_panel, "depth", axis=0, tiled=True),
        lax.all_gather(factor_panel, "depth", axis=0, tiled=True),
    )
    half_piece = spread(half_panel, ("row", "col"), 0)
    lower_piece = spread(factor_panel, ("row", "col"), 0)
    update = contract(half_piece, lower_cols) + contract(lower_piece, half_cols)
    trailing_out = trailing - update
    return (trailing_out, panel_out, corner_out)


def solution(mesh):
    in_specs = (
        P("depth", ("row", "col")),
        P(("row", "col", "depth"), None),
        P(("row", "col", "depth"), None),
        P(("row", "col", "depth"), None),
        P(("row", "col", "depth"), None),
    )
    out_specs = (
        P("depth", ("row", "col")),
        P(("row", "col", "depth"), None),
        P(("row", "col", "depth"), None),
    )
    return jax.shard_map(body, mesh=mesh, in_specs=in_specs, out_specs=out_specs, check_vma=False)
```

profile of v0, /device:TPU:1, one launch (start us, length us, event | category | flops | bytes accessed | tf_op | source)
XLA Modules:
  0.0 346.5 jit_solution(1089525029329415944)
XLA Ops:
  8.0 0.0 copy-start
  8.0 0.0 all-gather.7.cloned.1.call-start
  8.1 1.4 maximum_bitcast_fusion
  9.5 0.0 all-gather.7.cloned.1.call-update
  9.5 0.0 all-reduce.7.cloned.1.call-start
  9.6 2.1 broadcast_select_fusion
  11.7 123.5 %all-gather.7.cloned.1.call-done = f32[256,4,2048]{2,1,0:T(4,128)} async-done(((f32[1,4,2048]{2,1,0:T(4,128)}), f32[256,4,2048]{2,1,0:T(4,128)}) %all-gather.7.cloned.1.call-update) | async-done | bytes 8388624 | tf_op jit(solution)/shard_map/all_gather | solution.py:13
  135.2 10.0 %reshape.7 = f32[1024,2048]{1,0:T(8,128)} reshape(f32[256,4,2048]{2,1,0:T(4,128)} %all-gather.7.cloned.1.call-done) | data formatting | bytes 16777216
  145.2 0.0 copy-start.1
  145.2 17.2 %fusion = f32[1024,1024]{1,0:T(8,128)S(1)} fusion(f32[1024,2048]{1,0:T(8,128)} %reshape.7), kind=kOutput, calls=%fused_computation | convolution fusion | flops 12884901888 | bytes 12582912 | tf_op jit(solution)/shard_map/dot_general | solution.py:28
  162.4 0.0 copy-done.1
  162.4 0.0 copy-start.2
  162.4 13.4 %fusion.2 = f32[1024,1024]{1,0:T(8,128)S(1)} fusion(f32[1024,1024]{1,0:T(8,128)S(1)} %fusion, f32[1024,2048]{1,0:T(8,128)S(1)} %copy-done.1), kind=kOutput, calls=%fused_computation.2 | convolution fusion | flops 12884901888 | bytes 12582912 | tf_op jit(solution)/shard_map/dot_general | solution.py:24
  175.9 0.0 copy-done.2
  175.9 0.0 copy-start.3
  175.9 3.4 fusion.14
  179.3 0.0 copy-done
  179.3 5.9 %fusion.15 = (f32[188,1024]{1,0:T(8,128)}, f32[188,1024]{1,0:T(8,128)}, f32[188,1024]{1,0:T(8,128)}) fusion(f32[188,1024]{1,0:T(8,128)S(1)} %fusion.14, pred[]{:T(512)S(6)} %eq.4, f32[188,1024]{1,0:T(8,128)S(1)} %copy-done, f32[1024,2048]{1,0:T(8,128)S(1)} %copy-done.1), kind=kOutput, calls=%fused_computation.17 | convolution fusion | flops 2366164992 | bytes 8077313 | tf_op jit(solution)/shard_map/dot_general | solution.py:28
  185.3 0.0 copy-done.3
  185.3 0.0 all-reduce.7.cloned.1.call-update
  185.3 0.0 all-gather.9.cloned.1.call-start
  185.4 0.5 all-gather.9.cloned.1.call-update
  185.9 0.0 all-reduce.5.cloned.1.call-start
  185.9 51.6 %all-reduce.7.cloned.1.call-done = (f32[188,1024]{1,0:T(8,128)}, f32[188,1024]{1,0:T(8,128)}) async-done(((f32[188,1024]{1,0:T(8,128)}, f32[188,1024]{1,0:T(8,128)}), (f32[188,1024]{1,0:T(8,128)}, f32[188,1024]{1,0:T(8,128)})) %all-reduce.7.cloned.1.call-update) | async-done | bytes 1540112 | tf_op jit(solution)/shard_map/psum | solution.py:19
  237.5 0.0 all-reduce.5.cloned.1.call-update
  237.5 0.0 all-gather.11.cloned.1.call-start
  237.6 0.5 all-gather.11.cloned.1.call-update
  238.1 0.0 all-gather.9.cloned.1.call-done
  238.2 6.0 %reshape.9 = f32[1504,1024]{1,0:T(8,128)} reshape(f32[8,188,1024]{2,1,0:T(8,128)} %all-gather.9.cloned.1.call-done) | data formatting | bytes 12320768
  244.1 1.4 constant_dynamic-slice_fusion
  245.5 69.4 %all-reduce.5.cloned.1.call-done = (f32[188,1024]{1,0:T(8,128)}, f32[188,1024]{1,0:T(8,128)}) async-done(((f32[188,1024]{1,0:T(8,128)}, f32[188,1024]{1,0:T(8,128)}), (f32[188,1024]{1,0:T(8,128)}, f32[188,1024]{1,0:T(8,128)})) %all-reduce.5.cloned.1.call-update) | async-done | bytes 1540112 | tf_op jit(solution)/shard_map/psum | solution.py:19
  314.9 8.6 %fusion.16 = f32[188,1504]{1,0:T(8,128)S(1)} fusion(f32[188,1024]{1,0:T(8,128)} %get-tuple-element.3, f32[1504,1024]{1,0:T(8,128)} %reshape.9), kind=kOutput, calls=%fused_computation.18 | convolution fusion | flops 3474456576 | bytes 8061440 | tf_op jit(solution)/shard_map/dot_general | solution.py:28
  323.5 0.0 copy-start.4
  323.5 0.0 all-gather.11.cloned.1.call-done
  323.6 6.0 %reshape.11 = f32[1504,1024]{1,0:T(8,128)} reshape(f32[8,188,1024]{2,1,0:T(8,128)} %all-gather.11.cloned.1.call-done) | data formatting | bytes 12320768
  329.6 0.0 copy-done.4
  329.6 9.7 %fusion.7 = f32[188,1504]{1,0:T(8,128)} fusion(f32[188,1504]{1,0:T(8,128)S(1)} %copy-done.4, f32[188,1504]{1,0:T(8,128)S(1)} %fusion.16, f32[188,1024]{1,0:T(8,128)} %get-tuple-element.4, f32[1504,1024]{1,0:T(8,128)} %reshape.11), kind=kOutput, calls=%fused_computation.8 | convolution fusion | flops 3475022080 | bytes 10323456 | tf_op jit(solution)/shard_map/dot_general | solution.py:28
Async XLA Ops:
  8.0 171.3 %copy-start = (f32[188,1024]{1,0:T(8,128)S(1)}, f32[188,1024]{1,0:T(8,128)}, u32[]{:S(2)}) copy-start(f32[188,1024]{1,0:T(8,128)} %param.6) | copy-start | bytes 2310148
  8.0 127.2 %all-gather.7.cloned.1.call-start = ((), (), s32[]{:S(2)}) async-start(), calls=%async_computation | async-start | bytes 8421376 | tf_op jit(solution)/shard_map/all_gather | solution.py:13
  9.5 228.0 %all-reduce.7.cloned.1.call-start = ((), (), s32[]{:S(2)}) async-start(), calls=%async_computation.4 | async-start | bytes 3145728 | tf_op jit(solution)/shard_map/psum | solution.py:19
  145.2 17.3 %copy-start.1 = (f32[1024,2048]{1,0:T(8,128)S(1)}, f32[1024,2048]{1,0:T(8,128)}, u32[]{:S(2)}) copy-start(f32[1024,2048]{1,0:T(8,128)} %reshape.7) | copy-start | bytes 25165828
  162.4 13.5 %copy-start.2 = (f32[188,1024]{1,0:T(8,128)S(1)}, f32[188,1024]{1,0:T(8,128)}, u32[]{:S(2)}) copy-start(f32[188,1024]{1,0:T(8,128)} %param.7) | copy-start | bytes 2310148
  175.9 9.4 %copy-start.3 = (f32[1024,1024]{1,0:T(8,128)}, f32[1024,1024]{1,0:T(8,128)S(1)}, u32[]{:S(2)}) copy-start(f32[1024,1024]{1,0:T(8,128)S(1)} %fusion.2) | copy-start | bytes 12582916
  185.3 52.8 %all-gather.9.cloned.1.call-start = ((), (), s32[]{:S(2)}) async-start(), calls=%async_computation.1 | async-start | bytes 7077888 | tf_op jit(solution)/shard_map/all_gather | solution.py:52
  185.9 129.0 %all-reduce.5.cloned.1.call-start = ((), (), s32[]{:S(2)}) async-start(), calls=%async_computation.3 | async-start | bytes 3145728 | tf_op jit(solution)/shard_map/psum | solution.py:19
  237.5 86.0 %all-gather.11.cloned.1.call-start = ((), (), s32[]{:S(2)}) async-start(), calls=%async_computation.2 | async-start | bytes 7077888 | tf_op jit(solution)/shard_map/all_gather | solution.py:51
  323.5 6.1 %copy-start.4 = (f32[188,1504]{1,0:T(8,128)S(1)}, f32[188,1504]{1,0:T(8,128)}, u32[]{:S(2)}) copy-start(f32[188,1504]{1,0:T(8,128)} %param.5) | copy-start | bytes 3393028
Sparse Core Ops, SparseCore 0:
  13.1 122.0 all-gather.6
  185.4 52.0 all-reduce.6
  239.9 74.9 all-reduce.4
Sparse Core Ops, SparseCore 1:
  187.6 40.2 all-gather.8
  239.9 43.8 all-gather.10
where the time goes:
time: 350 us; the launch traced here: 346 us
  waiting for transfers between devices  246 us (70%)
  matrix products  58.4 us (17%)
  local copies, waits for them, and re-layouts  23.4 us (7%)
  between operations  15.3 us (4%)
  other arithmetic  3.52 us (1%)
    all_gather x1, waiting for transfers between devices, sent_together(): lax.all_gather(both, axis, axis=dim, tiled=True)  124 us
    psum x2, waiting for transfers between devices, spread(): array = lax.psum(array, axis)  121 us
    dot_general x4, matrix products, contract(): lax.dot_general(left, right, (((1,), (1,)), ((), ())), precision=lax.Prec...  41.5 us
    unnamed x13, local copies, waits for them, and re-layouts  22 us
    dot_general x2, matrix products, matmul(): jnp.dot(left, right, precision=lax.Precision.HIGHEST, preferred_element_t...  16.9 us
  transfers between devices with their start and end apart: 5, of which 3 were waited for; matrix products, arithmetic and copies ran while one was open for 5% of the time, Pallas kernels for 0%

commit v1 on v0

v1 whole, which is shorter than its diff:
```python
import functools

import jax
import jax.numpy as jnp
from jax import lax
from jax.experimental import pallas as pl
from jax.experimental.pallas import tpu as pltpu
from jax.sharding import PartitionSpec as P

F32, BF16 = jnp.float32, jnp.bfloat16
MESH = pl.DeviceIdType.MESH
NN = (((1,), (0,)), ((), ()))
NT = (((1,), (1,)), ((), ()))


def split(x):
    hi = x.astype(BF16)
    return hi, (x - hi.astype(F32)).astype(BF16)


def dot(a, b, dims):
    return lax.dot_general(a, b, dims, preferred_element_type=F32)


def dot3(ah, al, bh, bl, dims):
    return dot(ah, bh, dims) + dot(ah, bl, dims) + dot(al, bh, dims)


class Ring:
    def __init__(self, n, me, axis, block, send, recv):
        self.n, self.me, self.axis, self.block = n, me, axis, block
        self.send, self.recv, self.steps = send, recv, n // 2

    def has(self, way, step, chunk):
        return step < self.steps or chunk == way

    def index(self, way, step, chunk):
        return (way * self.steps + step - 1) * 2 + chunk

    def copy(self, way, step, chunk, incoming=False):
        sign = 1 if way == 0 else -1
        hops = step if incoming else step - 1
        origin = lax.rem(self.me - sign * hops + self.n, self.n)
        target = lax.rem(self.me + sign + self.n, self.n)
        ref = self.block(origin, chunk)
        k = self.index(way, step, chunk)
        return pltpu.make_async_remote_copy(
            src_ref=ref, dst_ref=ref, send_sem=self.send.at[k], recv_sem=self.recv.at[k],
            device_id={self.axis: target}, device_id_type=MESH,
        )

    def order(self, step):
        keys = []
        for at in range(2):
            for way in range(2):
                chunk = at if way == 0 else 1 - at
                if self.has(way, step, chunk):
                    keys.append((way, step, chunk))
        return keys

    def start(self, step):
        for key in self.order(step):
            self.copy(*key).start()

    def arrived(self, way, step, chunk):
        self.copy(way, step, chunk, incoming=True).wait_recv()

    def forward(self, way, step, chunk):
        if step < self.steps and self.has(way, step + 1, chunk):
            self.copy(way, step + 1, chunk).start()

    def take(self, step, then=None):
        for key in self.order(step):
            self.arrived(*key)
            self.forward(*key)
            if then is not None:
                then(*key)

    def run(self):
        self.start(1)
        for step in range(1, self.steps + 1):
            self.take(step)

    def drain(self):
        for step in range(1, self.steps + 1):
            for key in self.order(step):
                self.copy(*key).wait_send()


def kernel(
    dims, trailing, a_in, f_in, s_in, w_in, t_out, p_out, c_out,
    rbuf, rhi, rlo, lsrc, lbuf, lhi, llo, mbuf, rows4, swap, whi, wlo, shi, slo, chi, clo,
    yhi, ylo, cblk, pq_hi, pq_lo, pbuf, ubuf, tbuf, cbuf,
    load, ysend, yrecv, rsend, rrecv, ms_send, ms_recv, mb_send, mb_recv, ls_send, ls_recv,
    lb_send, lb_recv, dr_send, dr_recv, dm_send, dm_recv, sw_send, sw_recv, sc_send, sc_recv,
):
    nx, nz, ny = dims
    nd = 2 * ny
    rows, width = a_in.shape
    whole = rows // 8 * 8
    x, z, depth = lax.axis_index("row"), lax.axis_index("col"), lax.axis_index("depth")
    y, core = depth // 2, lax.rem(depth, 2)
    lx, lz = lbuf.shape[1] // nx, width // nz
    half = width // 2
    other = y * 2 + 1 - core
    root = jnp.logical_and(x == 0, z == 0)

    def cols(chunk):
        return pl.ds(chunk * half, half)

    def remote(src, dst, send, recv, device):
        return pltpu.make_async_remote_copy(
            src_ref=src, dst_ref=dst, send_sem=send, recv_sem=recv, device_id=device, device_id_type=MESH
        )

    loads = [
        (w_in, rows4.at[0]),
        (s_in, rows4.at[1]),
        (a_in, rbuf.at[depth, 0]),
        (f_in, rbuf.at[depth, 1]),
        (a_in.at[pl.ds(0, whole)], lsrc.at[0, pl.ds(0, whole)]),
        (f_in.at[pl.ds(0, whole)], lsrc.at[1, pl.ds(0, whole)]),
        (trailing, tbuf),
    ]
    local = [pltpu.make_async_copy(src, dst, load.at[i]) for i, (src, dst) in enumerate(loads)]
    for copy in local:
        copy.start()

    barrier = pltpu.get_barrier_semaphore()
    peers = [{"depth": other}]
    peers += [{"depth": lax.rem(y + j, ny) * 2 + core} for j in range(1, ny)]
    peers += [{"col": lax.rem(z + 1, nz)}, {"col": lax.rem(z + nz - 1, nz)}]
    peers += [{"row": lax.rem(x + 1, nx)}, {"row": lax.rem(x + nx - 1, nx)}]
    for peer in peers:
        pl.semaphore_signal(barrier, inc=1, device_id=peer, device_id_type=MESH)

    @pl.when(root)
    def _():
        @pl.loop(1, nx * nz)
        def _(i):
            pl.semaphore_signal(barrier, inc=1, device_id={"row": i // nz, "col": lax.rem(i, nz)}, device_id_type=MESH)

    @pl.when(jnp.logical_not(root))
    def _():
        pl.semaphore_signal(barrier, inc=1, device_id={"row": 0, "col": 0}, device_id_type=MESH)

    for copy in local[:6]:
        copy.wait()
    lsrc[:, whole:rows] = rbuf[depth, :, whole:rows]

    @pl.when(root)
    def _():
        pl.semaphore_wait(barrier, len(peers) + nx * nz - 1)

    @pl.when(jnp.logical_not(root))
    def _():
        pl.semaphore_wait(barrier, len(peers) + 1)

    def mrings(who):
        if who == 0:
            small = Ring(nz, z, "col", lambda i, c: mbuf.at[0, x, i, :, cols(c)], ms_send, ms_recv)
            bulk = Ring(nx, x, "row", lambda i, c: mbuf.at[0, i, :, :, cols(c)], mb_send, mb_recv)
        else:
            small = Ring(nx, x, "row", lambda i, c: mbuf.at[1, i, z, :, cols(c)], ms_send, ms_recv)
            bulk = Ring(nz, z, "col", lambda i, c: mbuf.at[1, :, i, :, cols(c)], mb_send, mb_recv)
        return small, bulk

    def lpart(c, i, j):
        return lbuf.at[c, pl.ds(pl.multiple_of(i * lx, lx), lx), pl.ds(pl.multiple_of(j * lz, lz), lz)]

    def lrings(who):
        if who == 0:
            small = Ring(nz, z, "col", lambda i, c: lpart(c, x, i), ls_send, ls_recv)
            bulk = Ring(nx, x, "row", lambda i, c: lbuf.at[c, pl.ds(pl.multiple_of(i * lx, lx), lx)], lb_send, lb_recv)
        else:
            small = Ring(nx, x, "row", lambda i, c: lpart(c, i, z), ls_send, ls_recv)
            bulk = Ring(nz, z, "col", lambda i, c: lbuf.at[c, :, pl.ds(pl.multiple_of(i * lz, lz), lz)], lb_send, lb_recv)
        return small, bulk

    rring = Ring(ny, y, "depth_y", lambda i, c: rbuf.at[i * 2 + core, c], rsend, rrecv)

    def rcopy(way, step, chunk, incoming=False):
        sign = 1 if way == 0 else -1
        hops = step if incoming else step - 1
        origin = lax.rem(y - sign * hops + ny, ny)
        target = lax.rem(y + sign + ny, ny)
        k = rring.index(way, step, chunk)
        ref = rbuf.at[origin * 2 + core, chunk]
        return remote(ref, ref, rsend.at[k], rrecv.at[k], {"depth": target * 2 + core})

    rring.copy = rcopy

    def slot_relay(i, c, k, mine=True):
        ref = rbuf.at[i * 2 + (core if mine else 1 - core), c]
        return remote(ref, ref, dr_send.at[k], dr_recv.at[k], {"depth": other})

    def ring_origin(way, step):
        return lax.rem(y - (step if way == 0 else -step) + ny, ny)

    def rrelay(way, step, chunk, mine=True):
        return slot_relay(ring_origin(way, step), chunk, 2 + rring.index(way, step, chunk), mine)

    def mrelay(ring, way, step, chunk):
        origin = ring.me if step == 0 else lax.rem(ring.me - (step if way == 0 else -step) + ring.n, ring.n)
        ref = ring.block(origin, chunk)
        k = chunk if step == 0 else 2 + ring.index(way, step, chunk)
        return remote(ref, ref, dm_send.at[k], dm_recv.at[k], {"depth": other})

    def mkeys(ring):
        keys = [(0, 0, 0), (0, 0, 1)]
        for step in range(1, ring.steps + 1):
            keys += ring.order(step)
        return keys

    trade = remote(rows4.at[1 - core], swap, sw_send, sw_recv, {"depth": other})
    trade.start()
    for c in range(2):
        slot_relay(y, c, c).start()
    trade.wait_recv()
    own, got = rows4[core], swap[...]
    first = core == 0
    tile = jnp.concatenate([jnp.where(first, own, got), jnp.where(first, got, own)], axis=0)

    def mrow(i):
        return mbuf.at[core, x, z, pl.ds(pl.multiple_of(i * 8, 8), 8)]

    mbuf[core, x, z, pl.ds(pl.multiple_of(y * 8, 8), 8), :] = tile

    def piece(i, j):
        return (pl.ds(0, 2), pl.ds(pl.multiple_of(i * lx, lx), lx), pl.ds(pl.multiple_of(j * lz, lz), lz))

    def scatter(i, j):
        return remote(lsrc.at[piece(i, j)], lbuf.at[piece(i, j)], sc_send.at[i * nz + j], sc_recv, {"row": i, "col": j})

    def ycopy(j, incoming=False):
        ref = mrow(lax.rem(y + ny - j, ny) if incoming else y)
        return remote(ref, ref, ysend.at[j], yrecv.at[j], {"depth": lax.rem(y + j, ny) * 2 + core})

    for j in range(1, ny):
        ycopy(j).start()
    rring.start(1)

    @pl.when(root)
    def _():
        lbuf[:, 0:lx, 0:lz] = lsrc[:, 0:lx, 0:lz]

        @pl.loop(1, nx * nz)
        def _(i):
            scatter(i // nz, lax.rem(i, nz)).start()

    for j in range(1, ny):
        ycopy(j, incoming=True).wait_recv()

    def gather(who):
        small, bulk = mrings(who)
        lsmall, lbulk = lrings(who)
        small.run()
        bulk.start(1)
        for c in range(2):
            mrelay(bulk, 0, 0, c).start()

        @pl.when(jnp.logical_not(root))
        def _():
            scatter(x, z).wait_recv()

        lsmall.run()
        bulk.take(1, lambda *key: mrelay(bulk, *key).start())
        lbulk.start(1)
        for key in rring.order(1):
            rring.arrived(*key)
            rring.forward(*key)
            rrelay(*key).start()
        for step in range(2, bulk.steps + 1):
            bulk.take(step, lambda *key: mrelay(bulk, *key).start())
        for step in range(1, lbulk.steps + 1):
            lbulk.take(step)
        theirs = mrings(1 - who)[1]
        for key in mkeys(theirs):
            mrelay(theirs, *key).wait_recv()

    for who in range(2):
        @pl.when(core == who)
        def _():
            gather(who)

    block = mbuf.shape[3]

    @pl.loop(0, nx * nz)
    def _(i):
        at = pl.ds(pl.multiple_of(i * block, block), block)
        whi[at], wlo[at] = split(mbuf[0, i // nz, lax.rem(i, nz)])
        shi[at], slo[at] = split(mbuf[1, i // nz, lax.rem(i, nz)])

    tile_rows = yhi.shape[0]
    nt = half

    @pl.loop(0, width // tile_rows)
    def _(i):
        at = pl.ds(pl.multiple_of(i * tile_rows, tile_rows), tile_rows)

        @pl.loop(0, width // nt)
        def _(j):
            to = pl.ds(pl.multiple_of(j * nt, nt), nt)
            yhi[:, to], ylo[:, to] = split(dot3(whi[at], wlo[at], shi[:, to], slo[:, to], NN))

        @pl.loop(0, width // nt)
        def _(j):
            to = pl.ds(pl.multiple_of(j * nt, nt), nt)
            out = dot3(yhi[...], ylo[...], whi[to], wlo[to], NT)
            cblk[:, to] = out
            chi[at, to], clo[at, to] = split(out)

        chip = (x * nz + z) * ny + y

        @pl.when(chip // (tile_rows // 8) == i)
        def _():
            mine = cblk[pl.ds(pl.multiple_of(lax.rem(chip, tile_rows // 8) * 8, 8), 8), :]
            cbuf[...] = jnp.where(first, mine[0:4], mine[4:8])

    c_copy = pltpu.make_async_copy(cbuf, c_out, load.at[0])
    c_copy.start()

    def split_rows(i):
        for c in range(2):
            rhi[i, c, 0:rows], rlo[i, c, 0:rows] = split(rbuf[i, c])

    split_rows(depth)
    for c in range(2):
        lhi[c], llo[c] = split(lbuf[c])

    @pl.loop(0, width // nt)
    def _(j):
        to = pl.ds(pl.multiple_of(j * nt, nt), nt)
        out = dot3(rhi[depth, 0], rlo[depth, 0], whi[to], wlo[to], NT)
        out = out - dot3(rhi[depth, 1], rlo[depth, 1], chi[:, to], clo[:, to], NN)
        pbuf[:, to] = out[0:rows]
        out = dot3(lhi[0], llo[0], whi[to], wlo[to], NT)
        out = out - dot3(lhi[1], llo[1], chi[:, to], clo[:, to], NN)
        pq_hi[1, :, to], pq_lo[1, :, to] = split(out)
        out = dot3(lhi[1], llo[1], whi[:, to], wlo[:, to], NN)
        pq_hi[0, :, to], pq_lo[0, :, to] = split(out)

    p_copy = pltpu.make_async_copy(pbuf, p_out, load.at[1])
    p_copy.start()

    for step in range(2, rring.steps + 1):
        for key in rring.order(step):
            rring.arrived(*key)
            rrelay(*key).start()
    for c in range(2):
        slot_relay(y, c, c, mine=False).wait_recv()
    for step in range(1, rring.steps + 1):
        for key in rring.order(step):
            rrelay(*key, mine=False).wait_recv()

    @pl.loop(0, nd)
    def _(i):
        @pl.when(i != depth)
        def _():
            split_rows(i)

        out = dot3(pq_hi[0], pq_lo[0], rhi[i, 0], rlo[i, 0], NT)
        ubuf[i, :, 0:rhi.shape[2]] = out + dot3(pq_hi[1], pq_lo[1], rhi[i, 1], rlo[i, 1], NT)

    local[6].wait()

    def rest(at):
        update = jnp.concatenate([ubuf[i, at, 0:rows] for i in range(nd)], axis=1)
        tbuf[at, :] = tbuf[at, :] - update

    @pl.loop(0, rows // 8)
    def _(i):
        rest(pl.ds(pl.multiple_of(i * 8, 8), 8))

    rest(slice(whole, rows))
    t_copy = pltpu.make_async_copy(tbuf, t_out, load.at[2])
    t_copy.start()

    trade.wait_send()
    for c in range(2):
        slot_relay(y, c, c).wait_send()
    for j in range(1, ny):
        ycopy(j).wait_send()
    rring.drain()
    for step in range(1, rring.steps + 1):
        for key in rring.order(step):
            rrelay(*key).wait_send()

    @pl.when(root)
    def _():
        @pl.loop(1, nx * nz)
        def _(i):
            scatter(i // nz, lax.rem(i, nz)).wait_send()

    for who in range(2):
        @pl.when(core == who)
        def _():
            small, bulk = mrings(who)
            lsmall, lbulk = lrings(who)
            for ring in (small, bulk, lsmall, lbulk):
                ring.drain()
            for key in mkeys(bulk):
                mrelay(bulk, *key).wait_send()

    c_copy.wait()
    p_copy.wait()
    t_copy.wait()


def body(dims, trailing, panel_block, factor_panel, corner_block, corner_inverse):
    nx, nz, ny = dims
    nd = 2 * ny
    rows, width = panel_block.shape
    pad = -(-rows // (8 * nx)) * 8 * nx
    padded = -(-rows // 16) * 16
    pad = max(pad, padded)
    corner_rows = corner_block.shape[0]
    big = max(nx, nz)
    sems = pltpu.SemaphoreType.DMA
    vmem = pltpu.VMEM
    any_space = pl.BlockSpec(memory_space=pl.ANY)
    tile_rows = min(256, width // 2)
    scratch = [
        vmem((nd, 2, rows, width), F32),
        vmem((nd, 2, padded, width), BF16), vmem((nd, 2, padded, width), BF16),
        vmem((2, pad, width), F32), vmem((2, pad, width), F32),
        vmem((2, pad, width), BF16), vmem((2, pad, width), BF16),
        vmem((2, nx, nz, 8 * ny, width), F32),
        vmem((2, corner_rows, width), F32), vmem((corner_rows, width), F32),
        vmem((width, width), BF16), vmem((width, width), BF16),
        vmem((width, width), BF16), vmem((width, width), BF16),
        vmem((width, width), BF16), vmem((width, width), BF16),
        vmem((tile_rows, width), BF16), vmem((tile_rows, width), BF16),
        vmem((tile_rows, width), F32),
        vmem((2, pad, width), BF16), vmem((2, pad, width), BF16),
        vmem((rows, width), F32),
        vmem((nd, pad, 256), F32),
        vmem(trailing.shape, F32),
        vmem((corner_rows, width), F32),
        sems((7,)), sems((ny,)), sems((ny,)), sems((2 * ny,)), sems((2 * ny,)),
        *[sems((2 * big,)) for _ in range(8)],
        sems((2 * ny + 2,)), sems((2 * ny + 2,)), sems((2 * big + 2,)), sems((2 * big + 2,)),
        sems(()), sems(()), sems((nx * nz,)), sems(()),
    ]
    return pl.pallas_call(
        functools.partial(kernel, dims),
        out_shape=(
            jax.ShapeDtypeStruct(trailing.shape, F32),
            jax.ShapeDtypeStruct(panel_block.shape, F32),
            jax.ShapeDtypeStruct(corner_block.shape, F32),
        ),
        in_specs=[any_space] * 5,
        out_specs=(any_space,) * 3,
        scratch_shapes=scratch,
        compiler_params=pltpu.CompilerParams(
            collective_id=0, has_side_effects=True, vmem_limit_bytes=67_000_000
        ),
        name="panel_step",
    )(trailing, panel_block, factor_panel, corner_block, corner_inverse)


def solution(mesh):
    dims = (mesh.shape["row"], mesh.shape["col"], mesh.shape["depth"] // 2)
    columns = P("depth", ("row", "col"))
    spread = P(("row", "col", "depth"), None)
    return jax.shard_map(
        functools.partial(body, dims),
        mesh=mesh,
        in_specs=(columns, spread, spread, spread, spread),
        out_specs=(columns, spread, spread),
        check_vma=False,
    )
```

time: 350 us -> 119 us (0.34)
  waiting for transfers between devices: 246 us -> 0 us
  Pallas kernels: 0 us -> 114 us
  matrix products: 58.4 us -> 0 us
  local copies, waits for them, and re-layouts: 23.4 us -> 3.92 us
  between operations: 15.3 us -> 0.65 us
  other arithmetic: 3.52 us -> 0 us
    all_gather x3 -> x0, waiting for transfers between devices: 124 us -> none  [the longest x1 124 us: sent_together(): lax.all_gather(both, axis, axis=dim, tiled=True)]
    psum x2 -> x0, waiting for transfers between devices: 121 us -> none  [spread(): array = lax.psum(array, axis)]
    pallas_call x0 -> x1, Pallas kernels: none -> 114 us  [body(): pl.pallas_call(functools.partial(kernel, dims), out_shape=(jax.ShapeDtype...]
    dot_general x6 -> x0, matrix products: 58.4 us -> none  [the longest x4 41.5 us: contract(): lax.dot_general(left, right, (((1,), (1,)), ((), ())), precision=lax.Prec...]
    unnamed x13 -> x7, local copies, waits for them, and re-layouts: 22 us -> 3.92 us
  transfers between devices with their start and end apart: 5 -> 0, of which waited for: 3 -> 0; matrix products, arithmetic and copies ran while one was open for 5% -> 0% of each run, Pallas kernels for 0% -> 0%
where the time goes in v1:
time: 119 us
  Pallas kernels  114 us (96%)
  local copies, waits for them, and re-layouts  3.92 us (3%)
    pallas_call x1, Pallas kernels, body(): pl.pallas_call(functools.partial(kernel, dims), out_shape=(jax.ShapeDtype...  114 us
    unnamed x7, local copies, waits for them, and re-layouts  3.92 us

profile of v1, /device:TPU:1, one launch (start us, length us, event | category | flops | bytes accessed | tf_op | source)
XLA Modules:
  0.0 118.7 jit_solution(356267071993306182)
XLA Ops:
  0.6 114.1 %panel_step.1 = (f32[188,1504]{1,0:T(8,128)}, f32[188,1024]{1,0:T(8,128)}, f32[4,1024]{1,0:T(4,128)}) custom-call(f32[188,1504]{1,0:T(8,128)} %trailing.1, f32[188,1024]{1,0:T(8,128)} %a_in.1, f32[188,1024]{1,0:T(8,128)} %f_in.1, f32[4,1024]{1,0:T(4,128)} %s_in.1, f32[4,1024]{1,0:T(4,128)} %w_in.1), custom_call_target="tpu_custom_call" | custom-call | tf_op jit(solution)/shard_map/panel_step/pallas_call | solution.py:445
  114.8 0.0 copy-start
  114.8 2.4 %copy.11 = f32[188,1504]{1,0:T(8,128)} copy(f32[188,1504]{1,0:T(8,128)} %get-tuple-element.6) | data formatting | bytes 2262016
  117.2 0.0 copy-done
  117.2 0.0 copy-start.1
  117.2 0.9 copy.12
  118.1 0.0 copy-done.1
  118.1 0.6 copy.13
Async XLA Ops:
  114.8 2.4 %copy-start = (f32[188,1024]{1,0:T(8,128)S(1)}, f32[188,1024]{1,0:T(8,128)}, u32[]{:S(2)}) copy-start(f32[188,1024]{1,0:T(8,128)} %get-tuple-element.7) | copy-start | bytes 2310148
  117.2 0.9 copy-start.1

commit v2 on v0

v2 whole, which is shorter than its diff:
```python
import functools

import jax
import jax.numpy as jnp
from jax import lax
from jax.experimental import pallas as pl
from jax.experimental.pallas import tpu as pltpu
from jax.sharding import PartitionSpec as P

F32, BF16 = jnp.float32, jnp.bfloat16
MESH = pl.DeviceIdType.MESH
NN = (((1,), (0,)), ((), ()))
NT = (((1,), (1,)), ((), ()))


def split(x):
    hi = x.astype(BF16)
    return hi, (x - hi.astype(F32)).astype(BF16)


def dot3(a, b, dims):
    (ah, al), (bh, bl) = a, b
    dot = functools.partial(lax.dot_general, dimension_numbers=dims, preferred_element_type=F32)
    return dot(ah, bh) + dot(ah, bl) + dot(al, bh)


def remote(src, dst, send, recv, device):
    return pltpu.make_async_remote_copy(
        src_ref=src, dst_ref=dst, send_sem=send, recv_sem=recv, device_id=device, device_id_type=MESH
    )


class Direct:
    def __init__(self, n, me, device, block, send, recv):
        self.n, self.me, self.device, self.block, self.send, self.recv = n, me, device, block, send, recv

    def copy(self, j, incoming=False):
        ref = self.block(lax.rem(self.me + self.n - j, self.n) if incoming else self.me)
        return remote(ref, ref, self.send.at[j], self.recv.at[j], self.device(lax.rem(self.me + j, self.n)))

    def start(self):
        for j in sorted(range(1, self.n), key=lambda j: -min(j, self.n - j)):
            self.copy(j).start()

    def take(self):
        for j in range(1, self.n):
            self.copy(j, incoming=True).wait_recv()

    def drain(self):
        for j in range(1, self.n):
            self.copy(j).wait_send()


class Ring:
    def __init__(self, n, me, device, block, counts, send, recv):
        self.n, self.me, self.device, self.block, self.counts = n, me, device, block, counts
        self.send, self.recv, self.steps = send, recv, n // 2

    def keys(self, step):
        out = []
        for at in range(2):
            for way in range(2):
                chunk = at if way == 0 else 1 - at
                if step < self.steps or chunk == way:
                    out += [(way, step, chunk, piece) for piece in range(self.counts[chunk])]
        return out

    def index(self, way, step, chunk, piece):
        return ((way * self.steps + step - 1) * 2 + chunk) * 2 + piece

    def origin(self, way, hops):
        return lax.rem(self.me - (hops if way == 0 else -hops) + self.n, self.n)

    def copy(self, way, step, chunk, piece, incoming=False):
        ref = self.block(self.origin(way, step if incoming else step - 1), chunk, piece)
        target = lax.rem(self.me + (1 if way == 0 else -1) + self.n, self.n)
        k = self.index(way, step, chunk, piece)
        return remote(ref, ref, self.send.at[k], self.recv.at[k], self.device(target))

    def start(self):
        for key in self.keys(1):
            self.copy(*key).start()

    def take(self, step, then=None, keys=None):
        for key in self.keys(step) if keys is None else keys:
            way, step, chunk, piece = key
            self.copy(*key, incoming=True).wait_recv()
            if step < self.steps and (step + 1 < self.steps or chunk == way):
                self.copy(way, step + 1, chunk, piece).start()
            if then is not None:
                then(*key)

    def drain(self):
        for step in range(1, self.steps + 1):
            for key in self.keys(step):
                self.copy(*key).wait_send()


class Relay:
    def __init__(self, ring, theirs, device, send, recv):
        self.ring, self.theirs, self.device, self.send, self.recv = ring, theirs, device, send, recv

    def own(self):
        counts = self.ring.counts
        return [(0, 0, chunk, piece) for chunk in range(2) for piece in range(counts[chunk])]

    def copy(self, way, step, chunk, piece, incoming=False):
        ref = (self.theirs if incoming else self.ring.block)(self.ring.origin(way, step), chunk, piece)
        k = chunk * 2 + piece if step == 0 else 4 + self.ring.index(way, step, chunk, piece)
        return remote(ref, ref, self.send.at[k], self.recv.at[k], self.device)

    def start(self, *key):
        self.copy(*key).start()

    def start_own(self):
        for key in self.own():
            self.copy(*key).start()

    def take(self, *keys):
        for key in keys:
            self.copy(*key, incoming=True).wait_recv()

    def every(self):
        return self.own() + [key for step in range(1, self.ring.steps + 1) for key in self.ring.keys(step)]

    def drain(self):
        for key in self.every():
            self.copy(*key).wait_send()


def kernel(
    dims, trailing, a_in, f_in, s_in, w_in, t_out, p_out, c_out,
    rbuf, rhi, rlo, lsrc, lbuf, phi, plo, mbuf, rows4, swap, whi, wlo, shi, slo, yhi, ylo, chi, clo,
    qhi, qlo, pbuf, ubuf, tbuf, cbuf,
    load, ysend, yrecv, rsend, rrecv, xs_send, xs_recv, zs_send, zs_recv, zb_send, zb_recv, xb_send, xb_recv,
    ls_send, ls_recv, lb_send, lb_recv, dr_send, dr_recv, dz_send, dz_recv, dx_send, dx_recv,
    sw_send, sw_recv, lx_send, lx_recv, lz_send, lz_recv,
):
    nx, nz, ny = dims
    nd = 2 * ny
    rows, width = a_in.shape
    whole = rows // 8 * 8
    x, z, depth = lax.axis_index("row"), lax.axis_index("col"), lax.axis_index("depth")
    y, core = depth // 2, lax.rem(depth, 2)
    pad = lbuf.shape[1]
    lx, lz = pad // nx, width // nz
    unit, half = width // nx, width // 2
    on_edge, on_side = z == 0, x == 0
    root = jnp.logical_and(on_edge, on_side)
    partner = {"depth": y * 2 + 1 - core}

    def on_x(i):
        return {"row": i}

    def on_y(i):
        return {"depth": i * 2 + core}

    def on_z(i):
        return {"col": i}

    def tile(i, size):
        return pl.ds(pl.multiple_of(i * size, size), size)

    def line(c, i):
        return lsrc.at[c, tile(i, lx)], lbuf.at[c, tile(i, lx)]

    def lscatter(c, i):
        src, dst = line(c, i)
        return remote(src, dst, lx_send.at[c * nx + i], lx_recv.at[c], on_x(i))

    def part(c, j):
        return lbuf.at[c, tile(x, lx), tile(j, lz)]

    def zscatter(c, j):
        return remote(part(c, j), part(c, j), lz_send.at[c * nz + j], lz_recv.at[c], on_z(j))

    def lsmall(c, j, incoming=False):
        ref = part(c, lax.rem(z + nz - j, nz) if incoming else z)
        return remote(ref, ref, ls_send.at[c * nz + j], ls_recv.at[c * nz + j], on_z(lax.rem(z + j, nz)))

    def lsmall_sends(c, act):
        for j in range(1, nz):
            @pl.when(lax.rem(z + j, nz) != 0)
            def _():
                act(lsmall(c, j))

    def edge(c):
        @pl.when(on_edge)
        def _():
            @pl.when(jnp.logical_not(on_side))
            def _():
                lscatter(c, x).wait_recv()

            for j in range(1, nz):
                zscatter(c, j).start()
            lsmall_sends(c, lambda copy: copy.start())

    def inner(c):
        @pl.when(jnp.logical_not(on_edge))
        def _():
            zscatter(c, z).wait_recv()
            lsmall_sends(c, lambda copy: copy.start())

    def gathered(c):
        @pl.when(jnp.logical_not(on_edge))
        def _():
            for j in range(1, nz):
                lsmall(c, j, incoming=True).wait_recv()

        for key in lbulk.keys(1):
            if key[2] == c:
                lbulk.copy(*key).start()

    lbulk = Ring(nx, x, on_x, lambda i, chunk, piece: lbuf.at[chunk, tile(i, lx)], (1, 1), lb_send, lb_recv)

    loads = [
        (w_in, rows4.at[0]),
        (s_in, rows4.at[1]),
        (a_in, rbuf.at[depth, 0]),
        (f_in, rbuf.at[depth, 1]),
        (a_in.at[pl.ds(0, whole)], lsrc.at[0, pl.ds(0, whole)]),
        (f_in.at[pl.ds(0, whole)], lsrc.at[1, pl.ds(0, whole)]),
        (trailing, tbuf),
    ]
    local = [pltpu.make_async_copy(src, dst, load.at[i]) for i, (src, dst) in enumerate(loads)]
    for copy in local:
        copy.start()

    barrier = pltpu.get_barrier_semaphore()
    peers = [partner]
    peers += [on_y(lax.rem(y + j, ny)) for j in range(1, ny)]
    peers += [on_x(lax.rem(x + j, nx)) for j in range(1, nx)]
    peers += [on_z(lax.rem(z + j, nz)) for j in range(1, nz)]
    for peer in peers:
        pl.semaphore_signal(barrier, inc=1, device_id=peer, device_id_type=MESH)

    for copy in local[:6]:
        copy.wait()
    lsrc[:, whole:rows] = rbuf[depth, :, whole:rows]

    pl.semaphore_wait(barrier, len(peers))

    trade = remote(rows4.at[1 - core], swap, sw_send, sw_recv, partner)
    trade.start()

    def panel(who):
        return lambda i, chunk, piece: rbuf.at[i * 2 + who, chunk, :, pl.ds(piece * half, half)]

    rring = Ring(ny, y, on_y, panel(core), (2, 2), rsend, rrecv)
    rrelay = Relay(rring, panel(1 - core), partner, dr_send, dr_recv)

    def myrow(i):
        return mbuf.at[core, x, z, tile(i, 8)]

    ysmall = Direct(ny, y, on_y, myrow, ysend, yrecv)

    @pl.when(root)
    def _():
        for c in range(2):
            for i in range(1, nx):
                lscatter(c, i).start()
        lbuf[:, 0:lx] = lsrc[:, 0:lx]

    trade.wait_recv()
    own, got = rows4[core], swap[...]
    first = core == 0
    mbuf[core, x, z, tile(y, 8), :] = jnp.concatenate(
        [jnp.where(first, own, got), jnp.where(first, got, own)], axis=0
    )
    ysmall.start()
    rring.start()

    def split_slot(i):
        for c in range(2):
            rhi[i, c, 0:rows], rlo[i, c, 0:rows] = split(rbuf[i, c])

    split_slot(depth)
    for c in range(2):
        phi[c, 0:rows] = rhi[depth, c, 0:rows]
        plo[c, 0:rows] = rlo[depth, c, 0:rows]

    rest = pl.ds(unit, width - unit)
    xsmall = Direct(nx, x, on_x, lambda i: mbuf.at[core, i, z, :, rest], xs_send, xs_recv)
    zsmall = Direct(nz, z, on_z, lambda i: mbuf.at[core, x, i, :, pl.ds(0, unit)], zs_send, zs_recv)
    layout = ([nx - 1], list(range(nx - 2, 0, -1)))

    def zblock(who):
        def block(i, chunk, piece):
            at = layout[chunk][piece]
            return mbuf.at[who, at, i, :, pl.ds(unit, at * unit)]
        return block

    def xblock(who):
        return lambda i, chunk, piece: mbuf.at[who, i, pl.ds(chunk * (nz // 2), nz // 2), :, pl.ds(0, unit)]

    zbulk = Ring(nz, z, on_z, zblock(core), tuple(len(part) for part in layout), zb_send, zb_recv)
    zrelay = Relay(zbulk, zblock(1 - core), partner, dz_send, dz_recv)
    xbulk = Ring(nx, x, on_x, xblock(core), (1, 1), xb_send, xb_recv)
    xrelay = Relay(xbulk, xblock(1 - core), partner, dx_send, dx_recv)

    ysmall.take()
    xsmall.start()
    zsmall.start()
    rrelay.start_own()
    edge(0)
    xsmall.take()
    zbulk.start()
    zrelay.start_own()
    zsmall.take()
    xbulk.start()
    xrelay.start_own()
    inner(0)
    edge(1)
    zbulk.take(1, zrelay.start)
    xbulk.take(1, xrelay.start)
    inner(1)
    if zbulk.steps > 1:
        zbulk.take(2, zrelay.start)
    early = [key for key in rring.keys(1) if key[2] == key[0]]
    late = [key for key in rring.keys(1) if key[2] != key[0]]
    rring.take(1, rrelay.start, early)
    gathered(0)
    if zbulk.steps > 2:
        zbulk.take(3, zrelay.start)
    for step in range(2, xbulk.steps + 1):
        xbulk.take(step, xrelay.start)
    gathered(1)
    for step in range(4, zbulk.steps + 1):
        zbulk.take(step, zrelay.start)
    zrelay.take(*zrelay.every())
    xrelay.take(*xrelay.every())
    lbulk.take(1)
    block = mbuf.shape[3]

    @pl.loop(0, nx * nz)
    def _(i):
        at = tile(i, block)
        whi[at], wlo[at] = split(mbuf[0, i // nz, lax.rem(i, nz)])
        shi[at], slo[at] = split(mbuf[1, i // nz, lax.rem(i, nz)])

    def cut(i, j=None):
        return slice(i * unit, (i + 1 if j is None else j) * unit)

    def pair(hi, lo, *at):
        return hi[at], lo[at]

    for i in range(nx):
        for j in range(nx):
            out = 0.0
            top = min(j, i + 1)
            if top > 0:
                out = dot3(pair(whi, wlo, cut(i), cut(0, top)), pair(shi, slo, cut(j), cut(0, top)), NT)
            if j <= i:
                out = out + dot3(pair(whi, wlo, cut(i), cut(j, i + 1)), pair(shi, slo, cut(j, i + 1), cut(j)), NN)
            yhi[cut(i), cut(j)], ylo[cut(i), cut(j)] = split(out)
    for i in range(nx):
        for j in range(i + 1):
            out = dot3(pair(yhi, ylo, cut(i), cut(0, j + 1)), pair(whi, wlo, cut(j), cut(0, j + 1)), NT)
            chi[cut(i), cut(j)], clo[cut(i), cut(j)] = split(out)
    rring.take(1, rrelay.start, late)
    rrelay.take(*rrelay.own())
    rrelay.take(*rring.keys(1))
    far = 2 if ny > 2 else 0

    def near(i):
        return lax.rem(2 * y + nd - 2 + i, nd) if far else i

    @pl.loop(0, nd - far)
    def _(i):
        @pl.when(near(i) != depth)
        def _():
            split_slot(near(i))

    for step in range(2, lbulk.steps + 1):
        lbulk.take(step)
    for c in range(2):
        phi[c, pad:2 * pad], plo[c, pad:2 * pad] = split(lbuf[c])
    both = slice(0, 2 * pad)
    slab = slice(pad, 2 * pad)
    for j in range(nx):
        out = dot3(pair(phi, plo, 0, both, cut(0, j + 1)), pair(whi, wlo, cut(j), cut(0, j + 1)), NT)
        if j > 0:
            out = out - dot3(pair(phi, plo, 1, both, cut(0, j)), pair(chi, clo, cut(j), cut(0, j)), NT)
        out = out - dot3(pair(phi, plo, 1, both, cut(j, nx)), pair(chi, clo, cut(j, nx), cut(j)), NN)
        pbuf[:, cut(j)] = out[0:rows]
        qhi[1, :, cut(j)], qlo[1, :, cut(j)] = split(out[pad:2 * pad])
        out = dot3(pair(phi, plo, 1, slab, cut(j, nx)), pair(whi, wlo, cut(j, nx), cut(j)), NN)
        qhi[0, :, cut(j)], qlo[0, :, cut(j)] = split(out)

    p_copy = pltpu.make_async_copy(pbuf, p_out, load.at[1])
    p_copy.start()

    chip = (x * nz + z) * ny + y
    at = tile(chip // 2, 16)
    mine = jnp.concatenate(
        [
            dot3(pair(yhi, ylo, at, cut(0, j + 1)), pair(whi, wlo, cut(j), cut(0, j + 1)), NT)
            for j in range(nx)
        ],
        axis=1,
    )
    mine = jnp.where(lax.rem(chip, 2) == 0, mine[0:8], mine[8:16])
    cbuf[...] = jnp.where(first, mine[0:4], mine[4:8])
    c_copy = pltpu.make_async_copy(cbuf, c_out, load.at[0])
    c_copy.start()

    def slot(i):
        out = dot3(pair(qhi, qlo, 0), pair(rhi, rlo, i, 0), NT)
        ubuf[i, :, 0:rhi.shape[2]] = out + dot3(pair(qhi, qlo, 1), pair(rhi, rlo, i, 1), NT)

    @pl.loop(0, nd - far)
    def _(i):
        slot(near(i))

    for step in range(2, rring.steps + 1):
        rring.take(step, rrelay.start)
    for step in range(2, rring.steps + 1):
        rrelay.take(*rring.keys(step))
    if far:
        @pl.loop(0, far)
        def _(i):
            at = lax.rem(2 * y + nd // 2 + i, nd)
            split_slot(at)
            slot(at)

    local[6].wait()

    def finish(at):
        update = jnp.concatenate([ubuf[i, at, 0:rows] for i in range(nd)], axis=1)
        tbuf[at, :] = tbuf[at, :] - update

    step = 32
    if rows >= step:
        @pl.loop(0, rows // step)
        def _(i):
            finish(tile(i, step))

    finish(slice(rows // step * step, rows))
    t_copy = pltpu.make_async_copy(tbuf, t_out, load.at[2])
    t_copy.start()

    trade.wait_send()
    for each in (ysmall, xsmall, zsmall, rring, zbulk, xbulk, lbulk, rrelay, zrelay, xrelay):
        each.drain()
    for c in range(2):
        lsmall_sends(c, lambda copy: copy.wait_send())

    @pl.when(on_edge)
    def _():
        for c in range(2):
            for j in range(1, nz):
                zscatter(c, j).wait_send()

    @pl.when(root)
    def _():
        for c in range(2):
            for i in range(1, nx):
                lscatter(c, i).wait_send()

    c_copy.wait()
    p_copy.wait()
    t_copy.wait()


def body(dims, trailing, panel_block, factor_panel, corner_block, corner_inverse):
    nx, nz, ny = dims
    nd = 2 * ny
    rows, width = panel_block.shape
    pad = max(-(-rows // (8 * nx)) * 8 * nx, -(-rows // 16) * 16)
    corner_rows = corner_block.shape[0]
    vmem = pltpu.VMEM
    square = vmem((width, width), BF16)
    any_space = pl.BlockSpec(memory_space=pl.ANY)

    def sems(*counts):
        return [pltpu.SemaphoreType.DMA((n,)) for n in counts for _ in range(2)]

    scratch = [
        vmem((nd, 2, rows, width), F32),
        vmem((nd, 2, pad, width), BF16), vmem((nd, 2, pad, width), BF16),
        vmem((2, pad, width), F32), vmem((2, pad, width), F32),
        vmem((2, 2 * pad, width), BF16), vmem((2, 2 * pad, width), BF16),
        vmem((2, nx, nz, 8 * ny, width), F32),
        vmem((2, corner_rows, width), F32), vmem((corner_rows, width), F32),
        *[square] * 8,
        vmem((2, pad, width), BF16), vmem((2, pad, width), BF16),
        vmem((rows, width), F32),
        vmem((nd, pad, 256), F32),
        vmem(trailing.shape, F32),
        vmem((corner_rows, width), F32),
        pltpu.SemaphoreType.DMA((7,)),
        *sems(ny, 4 * ny, nx, nz, 4 * nz, 4 * nx, 2 * nz, 4 * nx, 4 * ny + 4, 4 * nz + 4, 4 * nx + 4),
        pltpu.SemaphoreType.DMA, pltpu.SemaphoreType.DMA,
        *sems(2 * nx, 2 * nz),
    ]
    return pl.pallas_call(
        functools.partial(kernel, dims),
        out_shape=(
            jax.ShapeDtypeStruct(trailing.shape, F32),
            jax.ShapeDtypeStruct(panel_block.shape, F32),
            jax.ShapeDtypeStruct(corner_block.shape, F32),
        ),
        in_specs=[any_space] * 5,
        out_specs=(any_space,) * 3,
        scratch_shapes=scratch,
        compiler_params=pltpu.CompilerParams(
            collective_id=0, has_side_effects=True, vmem_limit_bytes=67_000_000
        ),
        name="panel_step",
    )(trailing, panel_block, factor_panel, corner_block, corner_inverse)


def solution(mesh):
    dims = (mesh.shape["row"], mesh.shape["col"], mesh.shape["depth"] // 2)
    columns = P("depth", ("row", "col"))
    spread = P(("row", "col", "depth"), None)
    return jax.shard_map(
        functools.partial(body, dims),
        mesh=mesh,
        in_specs=(columns, spread, spread, spread, spread),
        out_specs=(columns, spread, spread),
        check_vma=False,
    )
```

time: 350 us -> 95.5 us (0.27)
  the two profiles are of different devices: /device:TPU:1 before, /device:TPU:16 now
where the time goes in v2:
time: 95.5 us; the launch traced here: 95.4 us
  Pallas kernels  90.8 us (95%)
  local copies, waits for them, and re-layouts  3.92 us (4%)
    pallas_call x1, Pallas kernels, body(): pl.pallas_call(functools.partial(kernel, dims), out_shape=(jax.ShapeDtype...  90.8 us
    unnamed x7, local copies, waits for them, and re-layouts  3.92 us

profile of v2, /device:TPU:16, one launch (start us, length us, event | category | flops | bytes accessed | tf_op | source)
XLA Modules:
  0.0 95.4 jit_solution(10984306843877960902)
XLA Ops:
  0.6 90.8 %panel_step.1 = (f32[188,1504]{1,0:T(8,128)}, f32[188,1024]{1,0:T(8,128)}, f32[4,1024]{1,0:T(4,128)}) custom-call(f32[188,1504]{1,0:T(8,128)} %trailing.1, f32[188,1024]{1,0:T(8,128)} %a_in.1, f32[188,1024]{1,0:T(8,128)} %f_in.1, f32[4,1024]{1,0:T(4,128)} %s_in.1, f32[4,1024]{1,0:T(4,128)} %w_in.1), custom_call_target="tpu_custom_call" | custom-call | tf_op jit(solution)/shard_map/panel_step/pallas_call | solution.py:496
  91.4 0.0 copy-start
  91.4 2.4 %copy.11 = f32[188,1504]{1,0:T(8,128)} copy(f32[188,1504]{1,0:T(8,128)} %get-tuple-element.6) | data formatting | bytes 2262016
  93.9 0.0 copy-done
  93.9 0.0 copy-start.1
  93.9 0.9 copy.12
  94.8 0.0 copy-done.1
  94.8 0.6 copy.13
Async XLA Ops:
  91.4 2.4 %copy-start = (f32[188,1024]{1,0:T(8,128)S(1)}, f32[188,1024]{1,0:T(8,128)}, u32[]{:S(2)}) copy-start(f32[188,1024]{1,0:T(8,128)} %get-tuple-element.7) | copy-start | bytes 2310148
  93.9 0.9 copy-start.1

commit v3 on v2

--- a/solution.py
+++ b/solution.py
@@ -77,12 +77,17 @@
         k = self.index(way, step, chunk, piece)
         return remote(ref, ref, self.send.at[k], self.recv.at[k], self.device(target))
 
-    def start(self):
+    def start(self, chunk=None):
         for key in self.keys(1):
-            self.copy(*key).start()
-
-    def take(self, step, then=None, keys=None):
+            if chunk in (None, key[2]):
+                self.copy(*key).start()
+
+    def take(self, step, then=None, keys=None, only=None):
+        if step > self.steps:
+            return
         for key in self.keys(step) if keys is None else keys:
+            if only not in (None, key[2]):
+                continue
             way, step, chunk, piece = key
             self.copy(*key, incoming=True).wait_recv()
             if step < self.steps and (step + 1 < self.steps or chunk == way):
@@ -130,7 +135,7 @@
 
 def kernel(
     dims, trailing, a_in, f_in, s_in, w_in, t_out, p_out, c_out,
-    rbuf, rhi, rlo, lsrc, lbuf, phi, plo, mbuf, rows4, swap, whi, wlo, shi, slo, yhi, ylo, chi, clo,
+    rbuf, rhi, rlo, lsrc, lline, lbuf, phi, plo, mbuf, rows4, swap, whi, wlo, shi, slo, yhi, ylo, chi, clo,
     qhi, qlo, pbuf, ubuf, tbuf, cbuf,
     load, ysend, yrecv, rsend, rrecv, xs_send, xs_recv, zs_send, zs_recv, zb_send, zb_recv, xb_send, xb_recv,
     ls_send, ls_recv, lb_send, lb_recv, dr_send, dr_recv, dz_send, dz_recv, dx_send, dx_recv,
@@ -161,28 +166,12 @@
     def tile(i, size):
         return pl.ds(pl.multiple_of(i * size, size), size)
 
-    def line(c, i):
-        return lsrc.at[c, tile(i, lx)], lbuf.at[c, tile(i, lx)]
-
     def lscatter(c, i):
-        src, dst = line(c, i)
-        return remote(src, dst, lx_send.at[c * nx + i], lx_recv.at[c], on_x(i))
-
-    def part(c, j):
-        return lbuf.at[c, tile(x, lx), tile(j, lz)]
+        return remote(lsrc.at[c, tile(i, lx)], lline.at[c], lx_send.at[c * nx + i], lx_recv.at[c], on_x(i))
 
     def zscatter(c, j):
-        return remote(part(c, j), part(c, j), lz_send.at[c * nz + j], lz_recv.at[c], on_z(j))
-
-    def lsmall(c, j, incoming=False):
-        ref = part(c, lax.rem(z + nz - j, nz) if incoming else z)
-        return remote(ref, ref, ls_send.at[c * nz + j], ls_recv.at[c * nz + j], on_z(lax.rem(z + j, nz)))
-
-    def lsmall_sends(c, act):
-        for j in range(1, nz):
-            @pl.when(lax.rem(z + j, nz) != 0)
-            def _():
-                act(lsmall(c, j))
+        at = tile(j, lz)
+        return remote(lline.at[c, :, at], lbuf.at[c, tile(x, lx), at], lz_send.at[c * nz + j], lz_recv.at[c], on_z(j))
 
     def edge(c):
         @pl.when(on_edge)
@@ -193,24 +182,16 @@
 
             for j in range(1, nz):
                 zscatter(c, j).start()
-            lsmall_sends(c, lambda copy: copy.start())
+            lbuf[c, tile(x, lx), 0:lz] = lline[c, :, 0:lz]
 
     def inner(c):
         @pl.when(jnp.logical_not(on_edge))
         def _():
             zscatter(c, z).wait_recv()
-            lsmall_sends(c, lambda copy: copy.start())
-
-    def gathered(c):
-        @pl.when(jnp.logical_not(on_edge))
-        def _():
-            for j in range(1, nz):
-                lsmall(c, j, incoming=True).wait_recv()
-
-        for key in lbulk.keys(1):
-            if key[2] == c:
-                lbulk.copy(*key).start()
-
+
+        lsmall.start(c)
+
+    lsmall = Ring(nz, z, on_z, lambda i, chunk, piece: lbuf.at[chunk, tile(x, lx), tile(i, lz)], (1, 1), ls_send, ls_recv)
     lbulk = Ring(nx, x, on_x, lambda i, chunk, piece: lbuf.at[chunk, tile(i, lx)], (1, 1), lb_send, lb_recv)
 
     loads = [
@@ -259,7 +240,7 @@
         for c in range(2):
             for i in range(1, nx):
                 lscatter(c, i).start()
-        lbuf[:, 0:lx] = lsrc[:, 0:lx]
+        lline[...] = lsrc[:, 0:lx]
 
     trade.wait_recv()
     own, got = rows4[core], swap[...]
@@ -281,7 +262,10 @@
 
     rest = pl.ds(unit, width - unit)
     xsmall = Direct(nx, x, on_x, lambda i: mbuf.at[core, i, z, :, rest], xs_send, xs_recv)
-    zsmall = Direct(nz, z, on_z, lambda i: mbuf.at[core, x, i, :, pl.ds(0, unit)], zs_send, zs_recv)
+    zsmall = Ring(
+        nz, z, on_z, lambda i, chunk, piece: mbuf.at[core, x, i, :, pl.ds(chunk * (unit // 2), unit // 2)], (1, 1),
+        zs_send, zs_recv,
+    )
     layout = ([nx - 1], list(range(nx - 2, 0, -1)))
 
     def zblock(who):
@@ -302,34 +286,42 @@
     xsmall.start()
     zsmall.start()
     rrelay.start_own()
+    zsmall.take(1)
     edge(0)
+    zsmall.take(2)
     xsmall.take()
     zbulk.start()
     zrelay.start_own()
-    zsmall.take()
+    for step in range(3, zsmall.steps + 1):
+        zsmall.take(step)
     xbulk.start()
     xrelay.start_own()
     inner(0)
     edge(1)
     zbulk.take(1, zrelay.start)
+    lsmall.take(1, only=0)
+    inner(1)
+    zbulk.take(2, zrelay.start)
+    lsmall.take(2, only=0)
+    lsmall.take(1, only=1)
     xbulk.take(1, xrelay.start)
-    inner(1)
-    if zbulk.steps > 1:
-        zbulk.take(2, zrelay.start)
     early = [key for key in rring.keys(1) if key[2] == key[0]]
     late = [key for key in rring.keys(1) if key[2] != key[0]]
     rring.take(1, rrelay.start, early)
-    gathered(0)
-    if zbulk.steps > 2:
-        zbulk.take(3, zrelay.start)
-    for step in range(2, xbulk.steps + 1):
-        xbulk.take(step, xrelay.start)
-    gathered(1)
-    for step in range(4, zbulk.steps + 1):
-        zbulk.take(step, zrelay.start)
+    zbulk.take(3, zrelay.start)
+    lsmall.take(3, only=0)
+    lsmall.take(2, only=1)
+    xbulk.take(2, xrelay.start)
+    lsmall.take(4, only=0)
+    lbulk.start(0)
+    lsmall.take(3, only=1)
+    zbulk.take(4, zrelay.start)
+    lsmall.take(4, only=1)
+    lbulk.start(1)
     zrelay.take(*zrelay.every())
     xrelay.take(*xrelay.every())
     lbulk.take(1)
+    rring.take(1, rrelay.start, late)
     block = mbuf.shape[3]
 
     @pl.loop(0, nx * nz)
@@ -357,7 +349,6 @@
         for j in range(i + 1):
             out = dot3(pair(yhi, ylo, cut(i), cut(0, j + 1)), pair(whi, wlo, cut(j), cut(0, j + 1)), NT)
             chi[cut(i), cut(j)], clo[cut(i), cut(j)] = split(out)
-    rring.take(1, rrelay.start, late)
     rrelay.take(*rrelay.own())
     rrelay.take(*rring.keys(1))
     far = 2 if ny > 2 else 0
@@ -375,21 +366,32 @@
         lbulk.take(step)
     for c in range(2):
         phi[c, pad:2 * pad], plo[c, pad:2 * pad] = split(lbuf[c])
-    both = slice(0, 2 * pad)
+    def panel_out(at, j):
+        out = dot3(pair(phi, plo, 0, at, cut(0, j + 1)), pair(whi, wlo, cut(j), cut(0, j + 1)), NT)
+        if j > 0:
+            out = out - dot3(pair(phi, plo, 1, at, cut(0, j)), pair(chi, clo, cut(j), cut(0, j)), NT)
+        return out - dot3(pair(phi, plo, 1, at, cut(j, nx)), pair(chi, clo, cut(j, nx), cut(j)), NN)
+
     slab = slice(pad, 2 * pad)
     for j in range(nx):
-        out = dot3(pair(phi, plo, 0, both, cut(0, j + 1)), pair(whi, wlo, cut(j), cut(0, j + 1)), NT)
-        if j > 0:
-            out = out - dot3(pair(phi, plo, 1, both, cut(0, j)), pair(chi, clo, cut(j), cut(0, j)), NT)
-        out = out - dot3(pair(phi, plo, 1, both, cut(j, nx)), pair(chi, clo, cut(j, nx), cut(j)), NN)
-        pbuf[:, cut(j)] = out[0:rows]
-        qhi[1, :, cut(j)], qlo[1, :, cut(j)] = split(out[pad:2 * pad])
+        qhi[1, :, cut(j)], qlo[1, :, cut(j)] = split(panel_out(slab, j))
         out = dot3(pair(phi, plo, 1, slab, cut(j, nx)), pair(whi, wlo, cut(j, nx), cut(j)), NN)
         qhi[0, :, cut(j)], qlo[0, :, cut(j)] = split(out)
 
+    def slot(i):
+        out = dot3(pair(qhi, qlo, 0), pair(rhi, rlo, i, 0), NT)
+        ubuf[i, :, 0:rhi.shape[2]] = out + dot3(pair(qhi, qlo, 1), pair(rhi, rlo, i, 1), NT)
+
+    @pl.loop(0, nd - far)
+    def _(i):
+        slot(near(i))
+
+    for step in range(2, rring.steps + 1):
+        rring.take(step, rrelay.start)
+    for j in range(nx):
+        pbuf[:, cut(j)] = panel_out(slice(0, pad), j)[0:rows]
     p_copy = pltpu.make_async_copy(pbuf, p_out, load.at[1])
     p_copy.start()
-
     chip = (x * nz + z) * ny + y
     at = tile(chip // 2, 16)
     mine = jnp.concatenate(
@@ -403,17 +405,6 @@
     cbuf[...] = jnp.where(first, mine[0:4], mine[4:8])
     c_copy = pltpu.make_async_copy(cbuf, c_out, load.at[0])
     c_copy.start()
-
-    def slot(i):
-        out = dot3(pair(qhi, qlo, 0), pair(rhi, rlo, i, 0), NT)
-        ubuf[i, :, 0:rhi.shape[2]] = out + dot3(pair(qhi, qlo, 1), pair(rhi, rlo, i, 1), NT)
-
-    @pl.loop(0, nd - far)
-    def _(i):
-        slot(near(i))
-
-    for step in range(2, rring.steps + 1):
-        rring.take(step, rrelay.start)
     for step in range(2, rring.steps + 1):
         rrelay.take(*rring.keys(step))
     if far:
@@ -440,11 +431,8 @@
     t_copy.start()
 
     trade.wait_send()
-    for each in (ysmall, xsmall, zsmall, rring, zbulk, xbulk, lbulk, rrelay, zrelay, xrelay):
+    for each in (ysmall, xsmall, zsmall, lsmall, rring, zbulk, xbulk, lbulk, rrelay, zrelay, xrelay):
         each.drain()
-    for c in range(2):
-        lsmall_sends(c, lambda copy: copy.wait_send())
-
     @pl.when(on_edge)
     def _():
         for c in range(2):
@@ -478,7 +466,7 @@
     scratch = [
         vmem((nd, 2, rows, width), F32),
         vmem((nd, 2, pad, width), BF16), vmem((nd, 2, pad, width), BF16),
-        vmem((2, pad, width), F32), vmem((2, pad, width), F32),
+        vmem((2, pad, width), F32), vmem((2, pad // nx, width), F32), vmem((2, pad, width), F32),
         vmem((2, 2 * pad, width), BF16), vmem((2, 2 * pad, width), BF16),
         vmem((2, nx, nz, 8 * ny, width), F32),
         vmem((2, corner_rows, width), F32), vmem((corner_rows, width), F32),
@@ -489,7 +477,7 @@
         vmem(trailing.shape, F32),
         vmem((corner_rows, width), F32),
         pltpu.SemaphoreType.DMA((7,)),
-        *sems(ny, 4 * ny, nx, nz, 4 * nz, 4 * nx, 2 * nz, 4 * nx, 4 * ny + 4, 4 * nz + 4, 4 * nx + 4),
+        *sems(ny, 4 * ny, nx, 4 * nz, 4 * nz, 4 * nx, 4 * nz, 4 * nx, 4 * ny + 4, 4 * nz + 4, 4 * nx + 4),
         pltpu.SemaphoreType.DMA, pltpu.SemaphoreType.DMA,
         *sems(2 * nx, 2 * nz),
     ]

time: 95.5 us -> 97 us (1.016)
  the two profiles are of different devices: /device:TPU:16 before, /device:TPU:1 now
where the time goes in v3:
time: 97 us; the launch traced here: 96.7 us
  Pallas kernels  92.1 us (95%)
  local copies, waits for them, and re-layouts  3.92 us (4%)
    pallas_call x1, Pallas kernels, body(): pl.pallas_call(functools.partial(kernel, dims), out_shape=(jax.ShapeDtype...  92.1 us
    unnamed x7, local copies, waits for them, and re-layouts  3.92 us

profile of v3, /device:TPU:1, one launch (start us, length us, event | category | flops | bytes accessed | tf_op | source)
XLA Modules:
  0.0 96.7 jit_solution(10692666198887388616)
XLA Ops:
  0.6 92.1 %panel_step.1 = (f32[188,1504]{1,0:T(8,128)}, f32[188,1024]{1,0:T(8,128)}, f32[4,1024]{1,0:T(4,128)}) custom-call(f32[188,1504]{1,0:T(8,128)} %trailing.1, f32[188,1024]{1,0:T(8,128)} %a_in.1, f32[188,1024]{1,0:T(8,128)} %f_in.1, f32[4,1024]{1,0:T(4,128)} %s_in.1, f32[4,1024]{1,0:T(4,128)} %w_in.1), custom_call_target="tpu_custom_call" | custom-call | tf_op jit(solution)/shard_map/panel_step/pallas_call | solution.py:484
  92.8 0.0 copy-start
  92.8 2.4 %copy.11 = f32[188,1504]{1,0:T(8,128)} copy(f32[188,1504]{1,0:T(8,128)} %get-tuple-element.6) | data formatting | bytes 2262016
  95.2 0.0 copy-done
  95.2 0.0 copy-start.1
  95.2 0.9 copy.12
  96.1 0.0 copy-done.1
  96.1 0.6 copy.13
Async XLA Ops:
  92.8 2.4 %copy-start = (f32[188,1024]{1,0:T(8,128)S(1)}, f32[188,1024]{1,0:T(8,128)}, u32[]{:S(2)}) copy-start(f32[188,1024]{1,0:T(8,128)} %get-tuple-element.7) | copy-start | bytes 2310148
  95.2 0.9 copy-start.1

commit v4 on v2

--- a/solution.py
+++ b/solution.py
@@ -312,10 +312,10 @@
     inner(0)
     edge(1)
     zbulk.take(1, zrelay.start)
-    xbulk.take(1, xrelay.start)
     inner(1)
     if zbulk.steps > 1:
         zbulk.take(2, zrelay.start)
+    xbulk.take(1, xrelay.start)
     early = [key for key in rring.keys(1) if key[2] == key[0]]
     late = [key for key in rring.keys(1) if key[2] != key[0]]
     rring.take(1, rrelay.start, early)
@@ -329,7 +329,7 @@
         zbulk.take(step, zrelay.start)
     zrelay.take(*zrelay.every())
     xrelay.take(*xrelay.every())
-    lbulk.take(1)
+    rring.take(1, rrelay.start, late)
     block = mbuf.shape[3]
 
     @pl.loop(0, nx * nz)
@@ -353,11 +353,11 @@
             if j <= i:
                 out = out + dot3(pair(whi, wlo, cut(i), cut(j, i + 1)), pair(shi, slo, cut(j, i + 1), cut(j)), NN)
             yhi[cut(i), cut(j)], ylo[cut(i), cut(j)] = split(out)
+    lbulk.take(1)
     for i in range(nx):
         for j in range(i + 1):
             out = dot3(pair(yhi, ylo, cut(i), cut(0, j + 1)), pair(whi, wlo, cut(j), cut(0, j + 1)), NT)
             chi[cut(i), cut(j)], clo[cut(i), cut(j)] = split(out)
-    rring.take(1, rrelay.start, late)
     rrelay.take(*rrelay.own())
     rrelay.take(*rring.keys(1))
     far = 2 if ny > 2 else 0
@@ -375,21 +375,32 @@
         lbulk.take(step)
     for c in range(2):
         phi[c, pad:2 * pad], plo[c, pad:2 * pad] = split(lbuf[c])
-    both = slice(0, 2 * pad)
+    def panel_out(at, j):
+        out = dot3(pair(phi, plo, 0, at, cut(0, j + 1)), pair(whi, wlo, cut(j), cut(0, j + 1)), NT)
+        if j > 0:
+            out = out - dot3(pair(phi, plo, 1, at, cut(0, j)), pair(chi, clo, cut(j), cut(0, j)), NT)
+        return out - dot3(pair(phi, plo, 1, at, cut(j, nx)), pair(chi, clo, cut(j, nx), cut(j)), NN)
+
     slab = slice(pad, 2 * pad)
     for j in range(nx):
-        out = dot3(pair(phi, plo, 0, both, cut(0, j + 1)), pair(whi, wlo, cut(j), cut(0, j + 1)), NT)
-        if j > 0:
-            out = out - dot3(pair(phi, plo, 1, both, cut(0, j)), pair(chi, clo, cut(j), cut(0, j)), NT)
-        out = out - dot3(pair(phi, plo, 1, both, cut(j, nx)), pair(chi, clo, cut(j, nx), cut(j)), NN)
-        pbuf[:, cut(j)] = out[0:rows]
-        qhi[1, :, cut(j)], qlo[1, :, cut(j)] = split(out[pad:2 * pad])
+        qhi[1, :, cut(j)], qlo[1, :, cut(j)] = split(panel_out(slab, j))
         out = dot3(pair(phi, plo, 1, slab, cut(j, nx)), pair(whi, wlo, cut(j, nx), cut(j)), NN)
         qhi[0, :, cut(j)], qlo[0, :, cut(j)] = split(out)
 
+    def slot(i):
+        out = dot3(pair(qhi, qlo, 0), pair(rhi, rlo, i, 0), NT)
+        ubuf[i, :, 0:rhi.shape[2]] = out + dot3(pair(qhi, qlo, 1), pair(rhi, rlo, i, 1), NT)
+
+    @pl.loop(0, nd - far)
+    def _(i):
+        slot(near(i))
+
+    for step in range(2, rring.steps + 1):
+        rring.take(step, rrelay.start)
+    for j in range(nx):
+        pbuf[:, cut(j)] = panel_out(slice(0, pad), j)[0:rows]
     p_copy = pltpu.make_async_copy(pbuf, p_out, load.at[1])
     p_copy.start()
-
     chip = (x * nz + z) * ny + y
     at = tile(chip // 2, 16)
     mine = jnp.concatenate(
@@ -403,17 +414,6 @@
     cbuf[...] = jnp.where(first, mine[0:4], mine[4:8])
     c_copy = pltpu.make_async_copy(cbuf, c_out, load.at[0])
     c_copy.start()
-
-    def slot(i):
-        out = dot3(pair(qhi, qlo, 0), pair(rhi, rlo, i, 0), NT)
-        ubuf[i, :, 0:rhi.shape[2]] = out + dot3(pair(qhi, qlo, 1), pair(rhi, rlo, i, 1), NT)
-
-    @pl.loop(0, nd - far)
-    def _(i):
-        slot(near(i))
-
-    for step in range(2, rring.steps + 1):
-        rring.take(step, rrelay.start)
     for step in range(2, rring.steps + 1):
         rrelay.take(*rring.keys(step))
     if far:

time: 95.5 us -> 91.3 us (0.956)
  the two profiles are of different devices: /device:TPU:16 before, /device:TPU:1 now
where the time goes in v4:
time: 91.3 us; the launch traced here: 91.1 us
  Pallas kernels  86.5 us (95%)
  local copies, waits for them, and re-layouts  3.92 us (4%)
    pallas_call x1, Pallas kernels, body(): pl.pallas_call(functools.partial(kernel, dims), out_shape=(jax.ShapeDtype...  86.5 us
    unnamed x7, local copies, waits for them, and re-layouts  3.92 us

profile of v4, /device:TPU:1, one launch (start us, length us, event | category | flops | bytes accessed | tf_op | source)
XLA Modules:
  0.0 91.1 jit_solution(4824442230429542058)
XLA Ops:
  0.6 86.5 %panel_step.1 = (f32[188,1504]{1,0:T(8,128)}, f32[188,1024]{1,0:T(8,128)}, f32[4,1024]{1,0:T(4,128)}) custom-call(f32[188,1504]{1,0:T(8,128)} %trailing.1, f32[188,1024]{1,0:T(8,128)} %a_in.1, f32[188,1024]{1,0:T(8,128)} %f_in.1, f32[4,1024]{1,0:T(4,128)} %s_in.1, f32[4,1024]{1,0:T(4,128)} %w_in.1), custom_call_target="tpu_custom_call" | custom-call | tf_op jit(solution)/shard_map/panel_step/pallas_call | solution.py:496
  87.2 0.0 copy-start
  87.2 2.4 %copy.11 = f32[188,1504]{1,0:T(8,128)} copy(f32[188,1504]{1,0:T(8,128)} %get-tuple-element.6) | data formatting | bytes 2262016
  89.6 0.0 copy-done
  89.6 0.0 copy-start.1
  89.6 0.9 copy.12
  90.5 0.0 copy-done.1
  90.5 0.6 copy.13
Async XLA Ops:
  87.2 2.4 %copy-start = (f32[188,1024]{1,0:T(8,128)S(1)}, f32[188,1024]{1,0:T(8,128)}, u32[]{:S(2)}) copy-start(f32[188,1024]{1,0:T(8,128)} %get-tuple-element.7) | copy-start | bytes 2310148
  89.6 0.9 copy-start.1

commit v5 on v4

--- a/solution.py
+++ b/solution.py
@@ -371,32 +371,12 @@
         def _():
             split_slot(near(i))
 
-    for step in range(2, lbulk.steps + 1):
-        lbulk.take(step)
-    for c in range(2):
-        phi[c, pad:2 * pad], plo[c, pad:2 * pad] = split(lbuf[c])
     def panel_out(at, j):
         out = dot3(pair(phi, plo, 0, at, cut(0, j + 1)), pair(whi, wlo, cut(j), cut(0, j + 1)), NT)
         if j > 0:
             out = out - dot3(pair(phi, plo, 1, at, cut(0, j)), pair(chi, clo, cut(j), cut(0, j)), NT)
         return out - dot3(pair(phi, plo, 1, at, cut(j, nx)), pair(chi, clo, cut(j, nx), cut(j)), NN)
 
-    slab = slice(pad, 2 * pad)
-    for j in range(nx):
-        qhi[1, :, cut(j)], qlo[1, :, cut(j)] = split(panel_out(slab, j))
-        out = dot3(pair(phi, plo, 1, slab, cut(j, nx)), pair(whi, wlo, cut(j, nx), cut(j)), NN)
-        qhi[0, :, cut(j)], qlo[0, :, cut(j)] = split(out)
-
-    def slot(i):
-        out = dot3(pair(qhi, qlo, 0), pair(rhi, rlo, i, 0), NT)
-        ubuf[i, :, 0:rhi.shape[2]] = out + dot3(pair(qhi, qlo, 1), pair(rhi, rlo, i, 1), NT)
-
-    @pl.loop(0, nd - far)
-    def _(i):
-        slot(near(i))
-
-    for step in range(2, rring.steps + 1):
-        rring.take(step, rrelay.start)
     for j in range(nx):
         pbuf[:, cut(j)] = panel_out(slice(0, pad), j)[0:rows]
     p_copy = pltpu.make_async_copy(pbuf, p_out, load.at[1])
@@ -414,6 +394,26 @@
     cbuf[...] = jnp.where(first, mine[0:4], mine[4:8])
     c_copy = pltpu.make_async_copy(cbuf, c_out, load.at[0])
     c_copy.start()
+    for step in range(2, lbulk.steps + 1):
+        lbulk.take(step)
+    for c in range(2):
+        phi[c, pad:2 * pad], plo[c, pad:2 * pad] = split(lbuf[c])
+    slab = slice(pad, 2 * pad)
+    for j in range(nx):
+        qhi[1, :, cut(j)], qlo[1, :, cut(j)] = split(panel_out(slab, j))
+        out = dot3(pair(phi, plo, 1, slab, cut(j, nx)), pair(whi, wlo, cut(j, nx), cut(j)), NN)
+        qhi[0, :, cut(j)], qlo[0, :, cut(j)] = split(out)
+
+    for step in range(2, rring.steps + 1):
+        rring.take(step, rrelay.start)
+    def slot(i):
+        out = dot3(pair(qhi, qlo, 0), pair(rhi, rlo, i, 0), NT)
+        ubuf[i, :, 0:rhi.shape[2]] = out + dot3(pair(qhi, qlo, 1), pair(rhi, rlo, i, 1), NT)
+
+    @pl.loop(0, nd - far)
+    def _(i):
+        slot(near(i))
+
     for step in range(2, rring.steps + 1):
         rrelay.take(*rring.keys(step))
     if far:

time: 91.3 us -> 88.4 us (0.968); the launches traced: 91.1 us -> 87.2 us
  Pallas kernels: 86.5 us -> 82.7 us
    pallas_call x1, Pallas kernels: 86.5 us -> 82.7 us  [body(): pl.pallas_call(functools.partial(kernel, dims), out_shape=(jax.ShapeDtype...]
where the time goes in v5:
time: 88.4 us; the launch traced here: 87.2 us
  Pallas kernels  82.7 us (94%)
  local copies, waits for them, and re-layouts  3.92 us (4%)
    pallas_call x1, Pallas kernels, body(): pl.pallas_call(functools.partial(kernel, dims), out_shape=(jax.ShapeDtype...  82.7 us
    unnamed x7, local copies, waits for them, and re-layouts  3.92 us

profile of v5, /device:TPU:1, one launch (start us, length us, event | category | flops | bytes accessed | tf_op | source)
XLA Modules:
  0.0 87.2 jit_solution(18241523152809958788)
XLA Ops:
  0.6 82.7 %panel_step.1 = (f32[188,1504]{1,0:T(8,128)}, f32[188,1024]{1,0:T(8,128)}, f32[4,1024]{1,0:T(4,128)}) custom-call(f32[188,1504]{1,0:T(8,128)} %trailing.1, f32[188,1024]{1,0:T(8,128)} %a_in.1, f32[188,1024]{1,0:T(8,128)} %f_in.1, f32[4,1024]{1,0:T(4,128)} %s_in.1, f32[4,1024]{1,0:T(4,128)} %w_in.1), custom_call_target="tpu_custom_call" | custom-call | tf_op jit(solution)/shard_map/panel_step/pallas_call | solution.py:496
  83.3 0.0 copy-start
  83.3 2.4 %copy.11 = f32[188,1504]{1,0:T(8,128)} copy(f32[188,1504]{1,0:T(8,128)} %get-tuple-element.6) | data formatting | bytes 2262016
  85.7 0.0 copy-done
  85.7 0.0 copy-start.1
  85.7 0.9 %copy.12 = f32[188,1024]{1,0:T(8,128)} copy(f32[188,1024]{1,0:T(8,128)S(1)} %copy-done) | data formatting | bytes 1540096
  86.6 0.0 copy-done.1
  86.6 0.6 copy.13
Async XLA Ops:
  83.3 2.4 %copy-start = (f32[188,1024]{1,0:T(8,128)S(1)}, f32[188,1024]{1,0:T(8,128)}, u32[]{:S(2)}) copy-start(f32[188,1024]{1,0:T(8,128)} %get-tuple-element.7) | copy-start | bytes 2310148
  85.7 0.9 %copy-start.1 = (f32[4,1024]{1,0:T(4,128)S(1)}, f32[4,1024]{1,0:T(4,128)}, u32[]{:S(2)}) copy-start(f32[4,1024]{1,0:T(4,128)} %get-tuple-element.8) | copy-start | bytes 49156
